TPU v7x, 32 devices: a whole 2x2x4 slice. The times are simulated.
32 devices in a mesh: shard: 16 (over z, y, core), model: 2 (over x).
Axes of the slice: x: 2, y: 2, z: 4, core: 2. Of those that a mesh axis runs over, the one named last changes fastest.
Arguments:
- gradients: float32 [128, 128, 4096], P(None, 'shard', 'model'), may hold values from -6 to 6
- momentum: float32 [128, 128, 4096], P(None, 'shard', 'model'), may hold values from -6 to 6
- weights: float32 [128, 128, 4096], P(None, 'shard', 'model'), may hold values from -0.1875 to 0.1875
Outputs:
- new_weights: float32 [128, 128, 4096], P(None, 'shard', 'model')
- new_momentum: float32 [128, 128, 4096], P(None, 'shard', 'model')
All inputs are finite; a program needn't handle non-finite values.
Results may differ from a plain program's by a relative error of at most 0.0001.
Values sent between devices are 32-bit elements; how exact they have to be, the bound alone decides.
A program may use at most 128 MiB of HBM per device.

v0:
```python
import functools

import jax
import jax.numpy as jnp
from jax import lax
from jax.experimental import pallas as pl
from jax.experimental.pallas import tpu as pltpu
from jax.sharding import PartitionSpec as P

ITERS = 3
AHEAD = 2
BEHIND = 3

hold_rate = 0.9
learn_rate = 0.9
decay_rate = 0.1

MESH = pl.DeviceIdType.MESH


def dot(a, b, contract):
    return lax.dot_general(
        a,
        b,
        ((contract[0], contract[1]), ((), ())),
        precision=lax.Precision.HIGHEST,
        preferred_element_type=jnp.float32,
    )


def mul(a, b):
    return dot(a, b, ((1,), (0,)))


def mixer(gram, eye):
    total = jnp.sum(jnp.sum(gram * eye, axis=1, keepdims=True), axis=0, keepdims=True)
    scale = lax.rsqrt(total + 1e-06)
    a = gram * scale * scale
    q = None
    for step in range(ITERS):
        p = 3.4445 * eye + (-4.775 * a + 2.0315 * mul(a, a))
        q = p if q is None else mul(p, q)
        if step < ITERS - 1:
            a = mul(mul(p, a), p)
    return q * scale


def flipped(me, k, n):
    out, bit = 0, 1
    while bit < n:
        own = (me // bit) % 2
        out = out + bit * ((1 - own) if (k // bit) % 2 else own)
        bit *= 2
    return out


def step_kernel(
    n, models, grad_ref, mom_ref, weight_ref, out_ref, new_ref,
    x, gs, ms, ws, gram, peers, gload, mload, wload, send1, recv1, send2, recv2, gsend, grecv,
):
    me = lax.axis_index("shard")
    col = lax.axis_index("model")
    _, per, rows, cols = grad_ref.shape
    side = n * rows
    chunk = min(cols, 512)
    dests = [flipped(me, k, n) for k in range(1, n)]
    mine = pl.ds(pl.multiple_of(me * rows, rows), rows)

    def loads(c):
        slot = c % 2
        return (
            pltpu.make_async_copy(grad_ref.at[:, c], gs.at[slot], gload.at[slot]),
            pltpu.make_async_copy(mom_ref.at[:, c], ms.at[slot], mload.at[slot]),
        )

    def weight_load(c):
        slot = c % 2
        return pltpu.make_async_copy(weight_ref.at[:, c], ws.at[slot], wload.at[slot])

    def load(c):
        for copy in loads(c):
            copy.start()

    def make(c):
        for copy in loads(c):
            copy.wait()
        slot = c % 2

        def one(j, carry):
            new_ref[j, c] = hold_rate * ms[slot, j] + gs[slot, j]
            return carry

        lax.fori_loop(0, n, one, 0)

    def finish(c):
        got = out_ref.at[:, c]
        pltpu.make_async_copy(got, got, recv2.at[c]).wait()
        weight_load(c).wait()
        slot = c % 2

        def one(j, carry):
            out_ref[j, c] = (1.0 - learn_rate * decay_rate) * ws[slot, j] - learn_rate * out_ref[j, c]
            return carry

        lax.fori_loop(0, n, one, 0)

    def forth(c):
        for dest in dests:
            pltpu.make_async_remote_copy(
                src_ref=new_ref.at[dest, c],
                dst_ref=x.at[c, mine, :],
                send_sem=send1.at[c],
                recv_sem=recv1.at[c],
                device_id={"shard": dest},
                device_id_type=MESH,
            ).start()
        pltpu.make_async_copy(new_ref.at[me, c], x.at[c, mine, :], recv1.at[c]).start()

    def back(c):
        for dest in dests:
            theirs = pl.ds(pl.multiple_of(dest * rows, rows), rows)
            pltpu.make_async_remote_copy(
                src_ref=x.at[c, theirs, :],
                dst_ref=out_ref.at[me, c],
                send_sem=send2.at[c],
                recv_sem=recv2.at[c],
                device_id={"shard": dest},
                device_id_type=MESH,
            ).start()
        pltpu.make_async_copy(x.at[c, mine, :], out_ref.at[me, c], recv2.at[c]).start()

    barrier = pltpu.get_barrier_semaphore()
    for dest in dests:
        pl.semaphore_signal(barrier, inc=1, device_id={"shard": dest}, device_id_type=MESH)
    for step in range(1, models):
        pl.semaphore_signal(barrier, inc=1, device_id={"model": (col + step) % models}, device_id_type=MESH)
    for c in range(min(2, per)):
        load(c)
        weight_load(c).start()
    make(0)
    pl.semaphore_wait(barrier, n - 1 + models - 1)
    forth(0)
    for c in range(2, min(AHEAD + 2, per + 1)):
        if c < per:
            load(c)
        make(c - 1)
    for c in range(1, min(AHEAD, per)):
        forth(c)

    eye = (
        lax.broadcasted_iota(jnp.int32, (side, side), 0) == lax.broadcasted_iota(jnp.int32, (side, side), 1)
    ).astype(jnp.float32)

    def round_(c, carry):
        pltpu.make_async_copy(x.at[c], x.at[c], recv1.at[c]).wait()

        def part(k, total):
            piece = x[c, :, pl.ds(pl.multiple_of(k * chunk, chunk), chunk)]
            return total + dot(piece, piece, ((1,), (1,)))

        gram[c] = lax.fori_loop(0, cols // chunk, part, jnp.zeros((side, side), jnp.float32))

        @pl.when(c + AHEAD < per)
        def _():
            forth(c + AHEAD)

        copies = []
        for step in range(1, models):
            copy = pltpu.make_async_remote_copy(
                src_ref=gram.at[c],
                dst_ref=peers.at[step - 1, c],
                send_sem=gsend.at[step - 1, c],
                recv_sem=grecv.at[step - 1, c],
                device_id={"model": (col + step) % models},
                device_id_type=MESH,
            )
            copy.start()
            copies.append(copy)
        whole = gram[c]
        for step, copy in enumerate(copies):
            copy.wait()
            whole = whole + peers[step, c]
        q = mixer(whole, eye)

        def apply(k, carry):
            at = pl.ds(pl.multiple_of(k * chunk, chunk), chunk)
            x[c, :, at] = mul(q, x[c, :, at])
            return carry

        lax.fori_loop(0, cols // chunk, apply, 0)

        @pl.when(c + AHEAD + 1 < per)
        def _():
            make(c + AHEAD + 1)

        @pl.when(c + AHEAD + 2 < per)
        def _():
            load(c + AHEAD + 2)

        back(c)

        @pl.when(c >= BEHIND)
        def _():
            finish(c - BEHIND)

            @pl.when(c - BEHIND + 2 < per)
            def _():
                weight_load(c - BEHIND + 2).start()

        return carry

    lax.fori_loop(0, per, round_, 0)

    def drain(c, carry):
        sent = x.at[c, pl.ds(0, side - rows), :]
        pltpu.make_async_copy(sent, sent, send1.at[c]).wait()
        return carry

    lax.fori_loop(0, per, drain, 0)

    def last(c, carry):
        finish(c)

        @pl.when(c + 2 < per)
        def _():
            weight_load(c + 2).start()

        return carry

    lax.fori_loop(max(per - BEHIND, 0), per, last, 0)

    def drain_back(c, carry):
        sent = x.at[c, pl.ds(0, side - rows), :]
        pltpu.make_async_copy(sent, sent, send2.at[c]).wait()
        return carry

    lax.fori_loop(0, per, drain_back, 0)


def step_direct(gradients, momentum, weights, n, models):
    mats, rows, cols = gradients.shape
    per, side = mats // n, n * rows
    others = max(models - 1, 1)
    split = (n, per, rows, cols)
    placed = pltpu.VMEM(split, jnp.float32)
    out, new = pl.pallas_call(
        functools.partial(step_kernel, n, models),
        out_shape=(placed, placed),
        in_specs=[pl.BlockSpec(memory_space=pltpu.HBM)] * 3,
        out_specs=[pl.BlockSpec(memory_space=pltpu.VMEM)] * 2,
        scratch_shapes=[
            pltpu.VMEM((per, side, cols), jnp.float32),
            pltpu.VMEM((2, n, rows, cols), jnp.float32),
            pltpu.VMEM((2, n, rows, cols), jnp.float32),
            pltpu.VMEM((2, n, rows, cols), jnp.float32),
            pltpu.VMEM((per, side, side), jnp.float32),
            pltpu.VMEM((others, per, side, side), jnp.float32),
            pltpu.SemaphoreType.DMA((2,)),
            pltpu.SemaphoreType.DMA((2,)),
            pltpu.SemaphoreType.DMA((2,)),
            pltpu.SemaphoreType.DMA((per,)),
            pltpu.SemaphoreType.DMA((per,)),
            pltpu.SemaphoreType.DMA((per,)),
            pltpu.SemaphoreType.DMA((per,)),
            pltpu.SemaphoreType.DMA((others, per)),
            pltpu.SemaphoreType.DMA((others, per)),
        ],
        compiler_params=pltpu.CompilerParams(
            collective_id=0, has_side_effects=True, vmem_limit_bytes=40 * 1024 * 1024
        ),
    )(*(array.reshape(split) for array in (gradients, momentum, weights)))
    return out.reshape(gradients.shape), new.reshape(gradients.shape)


def exchange_plain(new_momentum):
    moved = lax.all_to_all(new_momentum, "shard", split_axis=0, concat_axis=1, tiled=True)
    gram = lax.psum(
        jnp.einsum("mik,mjk->mij", moved, moved, precision=lax.Precision.HIGHEST), "model"
    )
    eye = jnp.eye(gram.shape[-1], dtype=jnp.float32)
    q = jax.vmap(lambda g: mixer(g, eye))(gram)
    iterate = jnp.einsum("mij,mjk->mik", q, moved, precision=lax.Precision.HIGHEST)
    return lax.all_to_all(iterate, "shard", split_axis=1, concat_axis=0, tiled=True)


def body(n, models, gradients, momentum, weights):
    mats, rows, cols = gradients.shape
    size = mats * rows * cols * 4
    if n & (n - 1) == 0 and rows % 8 == 0 and cols % 128 == 0 and size <= 8 << 20 and mats // n > BEHIND:
        return step_direct(gradients, momentum, weights, n, models)
    new_momentum = hold_rate * momentum + gradients
    back = exchange_plain(new_momentum)
    new_weights = (1.0 - learn_rate * decay_rate) * weights - learn_rate * back
    return (new_weights, new_momentum)


def solution(mesh):
    placed = (P(None, "shard", "model"), P(None, "shard", "model"), P(None, "shard", "model"))
    return jax.shard_map(
        functools.partial(body, mesh.shape["shard"], mesh.shape["model"]),
        mesh=mesh,
        in_specs=placed,
        out_specs=(P(None, "shard", "model"), P(None, "shard", "model")),
        check_vma=False,
    )
```

profile of v0, /device:TPU:11, one launch (start us, length us, event | category | flops | bytes accessed | tf_op | source)
XLA Modules:
  0.0 375.2 jit_solution(1770476323068181512)
XLA Ops:
  0.6 367.8 %shard_map.50 = (f32[16,8,8,2048]{3,2,1,0:T(8,128)S(1)}, f32[16,8,8,2048]{3,2,1,0:T(8,128)S(1)}) custom-call(f32[16,8,8,2048]{3,2,1,0:T(8,128)} %bitcast.7, f32[16,8,8,2048]{3,2,1,0:T(8,128)} %bitcast.8, f32[16,8,8,2048]{3,2,1,0:T(8,128)} %bitcast.9), custom_call_target="tpu_custom_call" | custom-call | tf_op jit(solution)/shard_map/pallas_call | solution.py:246
  368.4 3.4 copy.7
  371.8 3.4 copy.8
where the time goes:
time: 377 us; the launch traced here: 375 us
  Pallas kernels  368 us (98%)
  local copies, waits for them, and re-layouts  6.8 us (2%)
    pallas_call x1, Pallas kernels, step_direct(): pl.pallas_call(functools.partial(step_kernel, n, models), out_shape=(plac...  368 us

commit v1 on v0

--- a/solution.py
+++ b/solution.py
@@ -54,16 +54,31 @@
     return out
 
 
+def partners(me, n):
+    if n < 4:
+        return [flipped(me, k, n) for k in range(1, n)]
+    part = n // 4
+    at, low = me // part, me % part
+    upper = at // 2
+    far, near, beside = 3 * (1 - upper), 2 - upper, at + 1 - 2 * (at % 2)
+    lows = [flipped(low, k, part) for k in range(part)]
+    across = [part * at + k for at in (far, near) for k in lows]
+    within = [part * beside + k for k in lows] + [part * at + k for k in lows[1:]]
+    order = [None] * (n - 1)
+    order[0::2], order[1::2] = across, within
+    return order
+
+
 def step_kernel(
-    n, models, grad_ref, mom_ref, weight_ref, out_ref, new_ref,
-    x, gs, ms, ws, gram, peers, gload, mload, wload, send1, recv1, send2, recv2, gsend, grecv,
+    n, models, grad_ref, mom_ref, weight_ref, out_ref, new_ref, wlast_ref,
+    x, gs, ms, ws, gram, peers, gload, mload, wload, lload, send1, recv1, send2, recv2, gsend, grecv,
 ):
     me = lax.axis_index("shard")
     col = lax.axis_index("model")
     _, per, rows, cols = grad_ref.shape
     side = n * rows
     chunk = min(cols, 512)
-    dests = [flipped(me, k, n) for k in range(1, n)]
+    dests = partners(me, n)
     mine = pl.ds(pl.multiple_of(me * rows, rows), rows)
 
     def loads(c):
@@ -76,6 +91,9 @@
     def weight_load(c):
         slot = c % 2
         return pltpu.make_async_copy(weight_ref.at[:, c], ws.at[slot], wload.at[slot])
+
+    def last_load():
+        return pltpu.make_async_copy(weight_ref.at[:, per - 1], wlast_ref, lload)
 
     def load(c):
         for copy in loads(c):
@@ -146,6 +164,7 @@
         make(c - 1)
     for c in range(1, min(AHEAD, per)):
         forth(c)
+    last_load().start()
 
     eye = (
         lax.broadcasted_iota(jnp.int32, (side, side), 0) == lax.broadcasted_iota(jnp.int32, (side, side), 1)
@@ -203,7 +222,7 @@
         def _():
             finish(c - BEHIND)
 
-            @pl.when(c - BEHIND + 2 < per)
+            @pl.when(c - BEHIND + 2 < per - 1)
             def _():
                 weight_load(c - BEHIND + 2).start()
 
@@ -221,13 +240,16 @@
     def last(c, carry):
         finish(c)
 
-        @pl.when(c + 2 < per)
+        @pl.when(c + 2 < per - 1)
         def _():
             weight_load(c + 2).start()
 
         return carry
 
-    lax.fori_loop(max(per - BEHIND, 0), per, last, 0)
+    lax.fori_loop(max(per - BEHIND, 0), per - 1, last, 0)
+    got = out_ref.at[:, per - 1]
+    pltpu.make_async_copy(got, got, recv2.at[per - 1]).wait()
+    last_load().wait()
 
     def drain_back(c, carry):
         sent = x.at[c, pl.ds(0, side - rows), :]
@@ -235,6 +257,31 @@
         return carry
 
     lax.fori_loop(0, per, drain_back, 0)
+
+
+def close_kernel(out_ref, new_ref, wlast_ref, weights_ref, momentum_ref, stage, sems):
+    n, per, _, _ = out_ref.shape
+    pieces = 4
+    copies = []
+    for k in range(pieces):
+        at = pl.ds(k * (n // pieces), n // pieces)
+        copies.append((new_ref.at[at], momentum_ref.at[at]))
+        early = pl.ds(0, per - 1)
+        copies.append((out_ref.at[at, early], weights_ref.at[at, early]))
+    copies = [pltpu.make_async_copy(src, dst, sems.at[k]) for k, (src, dst) in enumerate(copies)]
+    for copy in copies:
+        copy.start()
+
+    def one(j, carry):
+        stage[j] = (1.0 - learn_rate * decay_rate) * wlast_ref[j] - learn_rate * out_ref[j, per - 1]
+        return carry
+
+    lax.fori_loop(0, n, one, 0)
+    end = pltpu.make_async_copy(stage, weights_ref.at[:, per - 1], sems.at[2 * pieces])
+    end.start()
+    for copy in copies:
+        copy.wait()
+    end.wait()
 
 
 def step_direct(gradients, momentum, weights, n, models):
@@ -243,11 +290,12 @@
     others = max(models - 1, 1)
     split = (n, per, rows, cols)
     placed = pltpu.VMEM(split, jnp.float32)
-    out, new = pl.pallas_call(
+    slab = pltpu.VMEM((n, rows, cols), jnp.float32)
+    held = pl.pallas_call(
         functools.partial(step_kernel, n, models),
-        out_shape=(placed, placed),
+        out_shape=(placed, placed, slab),
         in_specs=[pl.BlockSpec(memory_space=pltpu.HBM)] * 3,
-        out_specs=[pl.BlockSpec(memory_space=pltpu.VMEM)] * 2,
+        out_specs=[pl.BlockSpec(memory_space=pltpu.VMEM)] * 3,
         scratch_shapes=[
             pltpu.VMEM((per, side, cols), jnp.float32),
             pltpu.VMEM((2, n, rows, cols), jnp.float32),
@@ -258,6 +306,7 @@
             pltpu.SemaphoreType.DMA((2,)),
             pltpu.SemaphoreType.DMA((2,)),
             pltpu.SemaphoreType.DMA((2,)),
+            pltpu.SemaphoreType.DMA,
             pltpu.SemaphoreType.DMA((per,)),
             pltpu.SemaphoreType.DMA((per,)),
             pltpu.SemaphoreType.DMA((per,)),
@@ -269,6 +318,14 @@
             collective_id=0, has_side_effects=True, vmem_limit_bytes=40 * 1024 * 1024
         ),
     )(*(array.reshape(split) for array in (gradients, momentum, weights)))
+    out, new = pl.pallas_call(
+        close_kernel,
+        out_shape=(jax.ShapeDtypeStruct(split, jnp.float32),) * 2,
+        in_specs=[pl.BlockSpec(memory_space=pltpu.VMEM)] * 3,
+        out_specs=[pl.BlockSpec(memory_space=pltpu.HBM)] * 2,
+        scratch_shapes=[pltpu.VMEM((n, rows, cols), jnp.float32), pltpu.SemaphoreType.DMA((9,))],
+        compiler_params=pltpu.CompilerParams(vmem_limit_bytes=4 * 1024 * 1024),
+    )(*(pltpu.with_memory_space_constraint(array, pltpu.VMEM) for array in held))
     return out.reshape(gradients.shape), new.reshape(gradients.shape)
 
 
@@ -286,7 +343,7 @@
 def body(n, models, gradients, momentum, weights):
     mats, rows, cols = gradients.shape
     size = mats * rows * cols * 4
-    if n & (n - 1) == 0 and rows % 8 == 0 and cols % 128 == 0 and size <= 8 << 20 and mats // n > BEHIND:
+    if n & (n - 1) == 0 and rows % 8 == 0 and cols % 128 == 0 and size <= 8 << 20 and mats // n > BEHIND and n % 4 == 0:
         return step_direct(gradients, momentum, weights, n, models)
     new_momentum = hold_rate * momentum + gradients
     back = exchange_plain(new_momentum)

time: 377 us -> 373 us (0.989)
  local copies, waits for them, and re-layouts: 6.8 us -> 0 us
  Pallas kernels: 368 us -> 372 us
    unnamed x2 -> x0, local copies, waits for them, and re-layouts: 6.8 us -> none
    pallas_call x0 -> x1, Pallas kernels: none -> 5.95 us  [step_direct(): pl.pallas_call(close_kernel, out_shape=(jax.ShapeDtypeStruct(split, jnp.f...]
where the time goes in v1:
time: 373 us; the launch traced here: 372 us
  Pallas kernels  372 us (100%)
    pallas_call x1, Pallas kernels, step_direct(): pl.pallas_call(functools.partial(step_kernel, n, models), out_shape=(plac...  366 us

profile of v1, /device:TPU:11, one launch (start us, length us, event | category | flops | bytes accessed | tf_op | source)
XLA Modules:
  0.0 372.4 jit_solution(1936849680557702607)
XLA Ops:
  0.6 365.8 %shard_map.50 = (f32[16,8,8,2048]{3,2,1,0:T(8,128)S(1)}, f32[16,8,8,2048]{3,2,1,0:T(8,128)S(1)}, f32[16,8,2048]{2,1,0:T(8,128)S(1)}) custom-call(f32[16,8,8,2048]{3,2,1,0:T(8,128)} %bitcast.5, f32[16,8,8,2048]{3,2,1,0:T(8,128)} %bitcast.6, f32[16,8,8,2048]{3,2,1,0:T(8,128)} %bitcast.7), custom_call_target="tpu_custom_call" | custom-call | tf_op jit(solution)/shard_map/pallas_call | solution.py:294
  366.4 6.0 %shard_map.51 = (f32[16,8,8,2048]{3,2,1,0:T(8,128)}, f32[16,8,8,2048]{3,2,1,0:T(8,128)}) custom-call(f32[16,8,8,2048]{3,2,1,0:T(8,128)S(1)} %get-tuple-element.7.out_ref, f32[16,8,8,2048]{3,2,1,0:T(8,128)S(1)} %get-tuple-element.8.new_ref, f32[16,8,2048]{2,1,0:T(8,128)S(1)} %get-tuple-element.9.wlast_ref), custom_call_target="tpu_custom_call" | custom-call | tf_op jit(solution)/shard_map/pallas_call | solution.py:321

commit v2 on v0

--- a/solution.py
+++ b/solution.py
@@ -8,8 +8,9 @@
 from jax.sharding import PartitionSpec as P
 
 ITERS = 3
-AHEAD = 2
-BEHIND = 3
+AHEAD = 4
+LATE = 3
+HELD = 1
 
 hold_rate = 0.9
 learn_rate = 0.9
@@ -54,16 +55,81 @@
     return out
 
 
+def quarters(me, n):
+    at = me // (n // 4)
+    upper = at // 2
+    return at, at + 1 - 2 * (at % 2), 2 - upper, 3 * (1 - upper)
+
+
+def members(me, n, quarter):
+    part = n // 4
+    return [part * quarter + flipped(me % part, k, part) for k in range(part)]
+
+
+def woven(first, second):
+    order = []
+    for k in range(max(len(first), len(second))):
+        order += first[k : k + 1] + second[k : k + 1]
+    return order
+
+
+def partners(me, n):
+    own, beside, near, far = (members(me, n, quarter) for quarter in quarters(me, n))
+    return woven(far + near, beside + own[1:])
+
+
+def signal(semaphore, dest):
+    pl.semaphore_signal(semaphore, inc=1, device_id={"shard": dest}, device_id_type=MESH)
+
+
+def greet(me, n, middle):
+    _, beside, near, _ = quarters(me, n)
+    barrier = pltpu.get_barrier_semaphore()
+
+    @pl.when(middle)
+    def _():
+        for dest in members(me, n, near) + members(me, n, beside):
+            signal(barrier, dest)
+
+    own = members(me, n, quarters(me, n)[0])
+    for dest in own[1:]:
+        signal(barrier, dest)
+    return barrier, len(own) * 2 - 1
+
+
+def enter(me, n, middle, inside):
+    @pl.when(jnp.logical_not(middle))
+    def _():
+        for dest in members(me, n, quarters(me, n)[1]):
+            signal(inside, dest)
+
+
+def pass_across(me, n, middle, inside, passed):
+    @pl.when(middle)
+    def _():
+        pl.semaphore_wait(inside, n // 4)
+        signal(passed, members(me, n, quarters(me, n)[2])[0])
+
+
+def pass_outward(me, n, middle, passed):
+    pl.semaphore_wait(passed, 1)
+
+    @pl.when(middle)
+    def _():
+        signal(passed, members(me, n, quarters(me, n)[1])[0])
+
+
 def step_kernel(
-    n, models, grad_ref, mom_ref, weight_ref, out_ref, new_ref,
-    x, gs, ms, ws, gram, peers, gload, mload, wload, send1, recv1, send2, recv2, gsend, grecv,
+    n, models, grad_ref, mom_ref, weight_ref, out_ref, new_ref, x,
+    gs, ms, ws, gram, peers, gload, mload, wload, qload, send1, recv1, send2, recv2, hsend, hrecv, gsend, grecv, inside, passed,
 ):
     me = lax.axis_index("shard")
     col = lax.axis_index("model")
     _, per, rows, cols = grad_ref.shape
+    early = out_ref.shape[1]
     side = n * rows
     chunk = min(cols, 512)
-    dests = [flipped(me, k, n) for k in range(1, n)]
+    dests = partners(me, n)
     mine = pl.ds(pl.multiple_of(me * rows, rows), rows)
 
     def loads(c):
@@ -92,9 +158,11 @@
 
         lax.fori_loop(0, n, one, 0)
 
+    def arrived(c, blocks, semaphore):
+        got = out_ref.at[pl.ds(0, blocks), c]
+        pltpu.make_async_copy(got, got, semaphore).wait()
+
     def finish(c):
-        got = out_ref.at[:, c]
-        pltpu.make_async_copy(got, got, recv2.at[c]).wait()
         weight_load(c).wait()
         slot = c % 2
 
@@ -104,7 +172,32 @@
 
         lax.fori_loop(0, n, one, 0)
 
+    def quarter_loads(k, quarter):
+        at = pl.ds(quarter * part, part)
+        return (
+            pltpu.make_async_copy(grad_ref.at[at, 0], gs.at[0, at], qload.at[0, k]),
+            pltpu.make_async_copy(mom_ref.at[at, 0], ms.at[0, at], qload.at[1, k]),
+        )
+
+    def quarter_make(k, quarter):
+        for copy in quarter_loads(k, quarter):
+            copy.wait()
+
+        def one(j, carry):
+            at = quarter * part + j
+            new_ref[at, 0] = hold_rate * ms[0, at] + gs[0, at]
+            return carry
+
+        lax.fori_loop(0, part, one, 0)
+
     def forth(c):
+        forth_to(c, dests)
+        forth_own(c)
+
+    def forth_own(c):
+        pltpu.make_async_copy(new_ref.at[me, c], x.at[c, mine, :], recv1.at[c]).start()
+
+    def forth_to(c, dests):
         for dest in dests:
             pltpu.make_async_remote_copy(
                 src_ref=new_ref.at[dest, c],
@@ -114,32 +207,51 @@
                 device_id={"shard": dest},
                 device_id_type=MESH,
             ).start()
-        pltpu.make_async_copy(new_ref.at[me, c], x.at[c, mine, :], recv1.at[c]).start()
-
-    def back(c):
+
+    def back_own(c):
+        pltpu.make_async_copy(x.at[c, mine, :], out_ref.at[me, c], recv2.at[c]).start()
+
+    def back_to(c, dests, left, landed):
         for dest in dests:
             theirs = pl.ds(pl.multiple_of(dest * rows, rows), rows)
             pltpu.make_async_remote_copy(
                 src_ref=x.at[c, theirs, :],
                 dst_ref=out_ref.at[me, c],
-                send_sem=send2.at[c],
-                recv_sem=recv2.at[c],
+                send_sem=left,
+                recv_sem=landed,
                 device_id={"shard": dest},
                 device_id_type=MESH,
             ).start()
-        pltpu.make_async_copy(x.at[c, mine, :], out_ref.at[me, c], recv2.at[c]).start()
-
-    barrier = pltpu.get_barrier_semaphore()
-    for dest in dests:
-        pl.semaphore_signal(barrier, inc=1, device_id={"shard": dest}, device_id_type=MESH)
+
+    part = n // 4
+    own, beside, near, far = quarters(me, n)
+    middle = (own == 1) | (own == 2)
+    lead = jnp.where(middle, near, beside)
+    third = jnp.where(middle, beside, near)
+    firsts = (lead, own, third, far)
+
+    barrier, count = greet(me, n, middle)
     for step in range(1, models):
         pl.semaphore_signal(barrier, inc=1, device_id={"model": (col + step) % models}, device_id_type=MESH)
+    for k, quarter in enumerate(firsts):
+        for copy in quarter_loads(k, quarter):
+            copy.start()
+    pl.semaphore_wait(barrier, count + models - 1)
+    enter(me, n, middle, inside)
+    quarter_make(0, lead)
+    forth_to(0, members(me, n, lead))
+    load(1)
+
+    pass_across(me, n, middle, inside, passed)
+    quarter_make(1, own)
+    forth_to(0, members(me, n, own)[1:])
+    forth_own(0)
+    pass_outward(me, n, middle, passed)
+    quarter_make(2, third)
+    quarter_make(3, far)
+    forth_to(0, woven(members(me, n, far), members(me, n, third)))
     for c in range(min(2, per)):
-        load(c)
         weight_load(c).start()
-    make(0)
-    pl.semaphore_wait(barrier, n - 1 + models - 1)
-    forth(0)
     for c in range(2, min(AHEAD + 2, per + 1)):
         if c < per:
             load(c)
@@ -197,15 +309,28 @@
         def _():
             load(c + AHEAD + 2)
 
-        back(c)
-
-        @pl.when(c >= BEHIND)
-        def _():
-            finish(c - BEHIND)
-
-            @pl.when(c - BEHIND + 2 < per)
-            def _():
-                weight_load(c - BEHIND + 2).start()
+        holding = jnp.logical_and(jnp.logical_not(middle), c >= early - HELD)
+
+        final = jnp.logical_and(middle, c == early - 1)
+
+        @pl.when(jnp.logical_and(c < early - 1, jnp.logical_not(holding)))
+        def _():
+            back_to(c, dests, send2.at[c], recv2.at[c])
+
+        @pl.when(final)
+        def _():
+            across = members(me, n, near) + members(me, n, far)
+            others = woven(across, members(me, n, beside) + members(me, n, own)[1:])
+            back_to(c, others, send2.at[c], recv2.at[c])
+
+        @pl.when(jnp.logical_and(c < early, holding))
+        def _():
+            others = woven(members(me, n, beside), members(me, n, own)[1:]) + members(me, n, near)
+            back_to(c, others, send2.at[c], recv2.at[c])
+
+        @pl.when(c < early)
+        def _():
+            back_own(c)
 
         return carry
 
@@ -219,57 +344,239 @@
     lax.fori_loop(0, per, drain, 0)
 
     def last(c, carry):
+        arrived(c, n, recv2.at[c])
         finish(c)
 
-        @pl.when(c + 2 < per)
+        @pl.when(c + 2 < early)
         def _():
             weight_load(c + 2).start()
 
         return carry
 
-    lax.fori_loop(max(per - BEHIND, 0), per, last, 0)
+    lax.fori_loop(0, early - HELD, last, 0)
+
+    outer = jnp.logical_not(middle)
+    ends = tuple(enumerate(range(early - HELD, early)))
+
+    def drained(c, blocks, semaphore):
+        sent = x.at[c, pl.ds(0, blocks * rows), :]
+        pltpu.make_async_copy(sent, sent, semaphore).wait()
+
+    @pl.when(middle)
+    def _():
+        for _, c in ends:
+            arrived(c, n, recv2.at[c])
+
+    @pl.when(outer)
+    def _():
+        for _, c in ends:
+            arrived(c, n - part, recv2.at[c])
+        for k, c in ends:
+            back_to(c, members(me, n, far), hsend.at[k], hrecv.at[k])
+        for k, c in ends:
+            arrived(c, part, hrecv.at[k])
+
+    for _, c in ends:
+        finish(c)
 
     def drain_back(c, carry):
-        sent = x.at[c, pl.ds(0, side - rows), :]
-        pltpu.make_async_copy(sent, sent, send2.at[c]).wait()
+        drained(c, n - 1, send2.at[c])
         return carry
 
-    lax.fori_loop(0, per, drain_back, 0)
+    lax.fori_loop(0, early - HELD, drain_back, 0)
+
+    @pl.when(middle)
+    def _():
+        for _, c in ends:
+            drained(c, n - 1, send2.at[c])
+
+    @pl.when(outer)
+    def _():
+        for k, c in ends:
+            drained(c, n - 1 - part, send2.at[c])
+            drained(c, part, hsend.at[k])
+
+
+def tail_kernel(
+    n, per, x, weight_ref, token_ref, out_ref, wlast_ref, ws, wload, send, recv, inside, passed,
+):
+    me = lax.axis_index("shard")
+    _, late, rows, cols = out_ref.shape
+    early = per - late
+    own, beside, near, far = quarters(me, n)
+    middle = (own == 1) | (own == 2)
+    lead = jnp.where(middle, near, beside)
+    third = jnp.where(middle, beside, near)
+
+    def held(c):
+        return wlast_ref if c == late - 1 else ws.at[c]
+
+    def weight_load(c):
+        return pltpu.make_async_copy(weight_ref.at[:, early + c], held(c), wload.at[c])
+
+    def back_to(c, dests):
+        for dest in dests:
+            pltpu.make_async_remote_copy(
+                src_ref=x.at[early + c, pl.ds(pl.multiple_of(dest * rows, rows), rows), :],
+                dst_ref=out_ref.at[me, c],
+                send_sem=send.at[c],
+                recv_sem=recv.at[c],
+                device_id={"shard": dest},
+                device_id_type=MESH,
+            ).start()
+
+    barrier, count = greet(me, n, middle)
+    pl.semaphore_wait(barrier, count)
+    enter(me, n, middle, inside)
+    for c in range(late - 1):
+        back_to(c, members(me, n, lead))
+    pass_across(me, n, middle, inside, passed)
+    pass_outward(me, n, middle, passed)
+    for c in range(late):
+        if c < late - 1:
+            back_to(c, woven(members(me, n, far), members(me, n, third)) + members(me, n, own)[1:])
+        else:
+            back_to(c, partners(me, n))
+        mine = x.at[early + c, pl.ds(pl.multiple_of(me * rows, rows), rows), :]
+        pltpu.make_async_copy(mine, out_ref.at[me, c], recv.at[c]).start()
+    for c in range(late):
+        weight_load(c).start()
+
+    for c in range(late):
+        got = out_ref.at[:, c]
+        pltpu.make_async_copy(got, got, recv.at[c]).wait()
+        weight_load(c).wait()
+        if c < late - 1:
+
+            def one(j, carry, c=c):
+                out_ref[j, c] = (1.0 - learn_rate * decay_rate) * ws[c, j] - learn_rate * out_ref[j, c]
+                return carry
+
+            lax.fori_loop(0, n, one, 0)
+    for c in range(late):
+        sent = x.at[early + c, pl.ds(0, (n - 1) * rows), :]
+        pltpu.make_async_copy(sent, sent, send.at[c]).wait()
+
+
+def write_kernel(out_ref, new_ref, weights_ref, momentum_ref, token_ref, sems):
+    n, early, _, _ = out_ref.shape
+    token_ref[...] = jnp.zeros_like(token_ref)
+    pieces = 4
+    copies = []
+    for k in range(pieces):
+        at = pl.ds(k * (n // pieces), n // pieces)
+        copies.append((new_ref.at[at], momentum_ref.at[at]))
+        copies.append((out_ref.at[at], weights_ref.at[at, pl.ds(0, early)]))
+    copies = [pltpu.make_async_copy(src, dst, sems.at[k]) for k, (src, dst) in enumerate(copies)]
+    for copy in copies:
+        copy.start()
+    for copy in copies:
+        copy.wait()
+
+
+def close_kernel(begun_ref, out_ref, wlast_ref, weights_ref, stage, sems):
+    n, late, _, _ = out_ref.shape
+    per = weights_ref.shape[1]
+    early = per - late
+    ready = pltpu.make_async_copy(
+        out_ref.at[:, pl.ds(0, late - 1)], weights_ref.at[:, pl.ds(early, late - 1)], sems.at[0]
+    )
+    ready.start()
+
+    def one(j, carry):
+        stage[j] = (1.0 - learn_rate * decay_rate) * wlast_ref[j] - learn_rate * out_ref[j, late - 1]
+        return carry
+
+    lax.fori_loop(0, n, one, 0)
+    end = pltpu.make_async_copy(stage, weights_ref.at[:, per - 1], sems.at[1])
+    end.start()
+    ready.wait()
+    end.wait()
+
+
+def kept(array):
+    return pltpu.with_memory_space_constraint(array, pltpu.VMEM)
 
 
 def step_direct(gradients, momentum, weights, n, models):
     mats, rows, cols = gradients.shape
     per, side = mats // n, n * rows
+    early = per - LATE
     others = max(models - 1, 1)
     split = (n, per, rows, cols)
-    placed = pltpu.VMEM(split, jnp.float32)
-    out, new = pl.pallas_call(
+    slab = (n, rows, cols)
+    vmem, hbm = pl.BlockSpec(memory_space=pltpu.VMEM), pl.BlockSpec(memory_space=pltpu.HBM)
+    whole = jax.ShapeDtypeStruct(split, jnp.float32)
+    weights = weights.reshape(split)
+    out, new, x = pl.pallas_call(
         functools.partial(step_kernel, n, models),
-        out_shape=(placed, placed),
-        in_specs=[pl.BlockSpec(memory_space=pltpu.HBM)] * 3,
-        out_specs=[pl.BlockSpec(memory_space=pltpu.VMEM)] * 2,
+        out_shape=(
+            pltpu.VMEM((n, early, rows, cols), jnp.float32),
+            pltpu.VMEM(split, jnp.float32),
+            pltpu.VMEM((per, side, cols), jnp.float32),
+        ),
+        in_specs=[hbm] * 3,
+        out_specs=[vmem] * 3,
         scratch_shapes=[
-            pltpu.VMEM((per, side, cols), jnp.float32),
-            pltpu.VMEM((2, n, rows, cols), jnp.float32),
-            pltpu.VMEM((2, n, rows, cols), jnp.float32),
-            pltpu.VMEM((2, n, rows, cols), jnp.float32),
+            pltpu.VMEM((2, *slab), jnp.float32),
+            pltpu.VMEM((2, *slab), jnp.float32),
+            pltpu.VMEM((2, *slab), jnp.float32),
             pltpu.VMEM((per, side, side), jnp.float32),
             pltpu.VMEM((others, per, side, side), jnp.float32),
             pltpu.SemaphoreType.DMA((2,)),
             pltpu.SemaphoreType.DMA((2,)),
             pltpu.SemaphoreType.DMA((2,)),
+            pltpu.SemaphoreType.DMA((2, 4)),
             pltpu.SemaphoreType.DMA((per,)),
             pltpu.SemaphoreType.DMA((per,)),
-            pltpu.SemaphoreType.DMA((per,)),
-            pltpu.SemaphoreType.DMA((per,)),
+            pltpu.SemaphoreType.DMA((early,)),
+            pltpu.SemaphoreType.DMA((early,)),
+            pltpu.SemaphoreType.DMA((HELD,)),
+            pltpu.SemaphoreType.DMA((HELD,)),
             pltpu.SemaphoreType.DMA((others, per)),
             pltpu.SemaphoreType.DMA((others, per)),
+            pltpu.SemaphoreType.REGULAR,
+            pltpu.SemaphoreType.REGULAR,
         ],
         compiler_params=pltpu.CompilerParams(
             collective_id=0, has_side_effects=True, vmem_limit_bytes=40 * 1024 * 1024
         ),
-    )(*(array.reshape(split) for array in (gradients, momentum, weights)))
-    return out.reshape(gradients.shape), new.reshape(gradients.shape)
+    )(gradients.reshape(split), momentum.reshape(split), weights)
+    begun, new, token = pl.pallas_call(
+        write_kernel,
+        out_shape=(whole, whole, pltpu.VMEM((8, 128), jnp.float32)),
+        in_specs=[vmem] * 2,
+        out_specs=[hbm, hbm, vmem],
+        scratch_shapes=[pltpu.SemaphoreType.DMA((8,))],
+        compiler_params=pltpu.CompilerParams(vmem_limit_bytes=4 * 1024 * 1024),
+    )(kept(out), kept(new))
+    out, wlast = pl.pallas_call(
+        functools.partial(tail_kernel, n, per),
+        out_shape=(pltpu.VMEM((n, LATE, rows, cols), jnp.float32), pltpu.VMEM(slab, jnp.float32)),
+        in_specs=[vmem, hbm, vmem],
+        out_specs=[vmem] * 2,
+        scratch_shapes=[
+            pltpu.VMEM((LATE - 1, *slab), jnp.float32),
+            pltpu.SemaphoreType.DMA((LATE,)),
+            pltpu.SemaphoreType.DMA((LATE,)),
+            pltpu.SemaphoreType.DMA((LATE,)),
+            pltpu.SemaphoreType.REGULAR,
+            pltpu.SemaphoreType.REGULAR,
+        ],
+        compiler_params=pltpu.CompilerParams(
+            collective_id=1, has_side_effects=True, vmem_limit_bytes=38 * 1024 * 1024
+        ),
+    )(kept(x), weights, kept(token))
+    done = pl.pallas_call(
+        close_kernel,
+        out_shape=whole,
+        in_specs=[hbm, vmem, vmem],
+        out_specs=hbm,
+        scratch_shapes=[pltpu.VMEM(slab, jnp.float32), pltpu.SemaphoreType.DMA((2,))],
+        input_output_aliases={0: 0},
+        compiler_params=pltpu.CompilerParams(vmem_limit_bytes=4 * 1024 * 1024),
+    )(begun, kept(out), kept(wlast))
+    return done.reshape(gradients.shape), new.reshape(gradients.shape)
 
 
 def exchange_plain(new_momentum):
@@ -286,7 +593,7 @@
 def body(n, models, gradients, momentum, weights):
     mats, rows, cols = gradients.shape
     size = mats * rows * cols * 4
-    if n & (n - 1) == 0 and rows % 8 == 0 and cols % 128 == 0 and size <= 8 << 20 and mats // n > BEHIND:
+    if n & (n - 1) == 0 and rows % 8 == 0 and cols % 128 == 0 and size <= 8 << 20 and mats // n > LATE + HELD and n % 4 == 0:
         return step_direct(gradients, momentum, weights, n, models)
     new_momentum = hold_rate * momentum + gradients
     back = exchange_plain(new_momentum)

time: 377 us -> 371 us (0.984)
  local copies, waits for them, and re-layouts: 6.8 us -> 0 us
    unnamed x2 -> x0, local copies, waits for them, and re-layouts: 6.8 us -> none
    pallas_call x1 -> x4, Pallas kernels: 368 us -> 370 us  [the longest x1 291 us: step_direct(): pl.pallas_call(functools.partial(step_kernel, n, models), out_shape=(pltp...]
where the time goes in v2:
time: 371 us
  Pallas kernels  370 us (100%)
    pallas_call x1, Pallas kernels, step_direct(): pl.pallas_call(functools.partial(step_kernel, n, models), out_shape=(pltp...  291 us
    pallas_call x1, Pallas kernels, step_direct(): pl.pallas_call(functools.partial(tail_kernel, n, per), out_shape=(pltpu.V...  72.9 us

profile of v2, /device:TPU:11, one launch (start us, length us, event | category | flops | bytes accessed | tf_op | source)
XLA Modules:
  0.0 371.1 jit_solution(10267112427274971831)
XLA Ops:
  0.6 290.8 %shard_map.50 = (f32[16,5,8,2048]{3,2,1,0:T(8,128)S(1)}, f32[16,8,8,2048]{3,2,1,0:T(8,128)S(1)}, f32[8,128,2048]{2,1,0:T(8,128)S(1)}) custom-call(f32[16,8,8,2048]{3,2,1,0:T(8,128)} %bitcast.7, f32[16,8,8,2048]{3,2,1,0:T(8,128)} %bitcast.8, f32[16,8,8,2048]{3,2,1,0:T(8,128)} %bitcast.5), custom_call_target="tpu_custom_call" | custom-call | tf_op jit(solution)/shard_map/pallas_call | solution.py:511
  291.5 5.0 %shard_map.51 = (f32[16,8,8,2048]{3,2,1,0:T(8,128)}, f32[16,8,8,2048]{3,2,1,0:T(8,128)}, f32[8,128]{1,0:T(8,128)S(1)}) custom-call(f32[16,5,8,2048]{3,2,1,0:T(8,128)S(1)} %get-tuple-element.10.out_ref, f32[16,8,8,2048]{3,2,1,0:T(8,128)S(1)} %get-tuple-element.11.new_ref), custom_call_target="tpu_custom_call" | custom-call | tf_op jit(solution)/shard_map/pallas_call | solution.py:545
  296.5 72.9 %shard_map.52 = (f32[16,3,8,2048]{3,2,1,0:T(8,128)S(1)}, f32[16,8,2048]{2,1,0:T(8,128)S(1)}) custom-call(f32[8,128,2048]{2,1,0:T(8,128)S(1)} %get-tuple-element.13.x, f32[16,8,8,2048]{3,2,1,0:T(8,128)} %bitcast.6, f32[8,128]{1,0:T(8,128)S(1)} %get-tuple-element.14.token_ref), custom_call_target="tpu_custom_call" | custom-call | tf_op jit(solution)/shard_map/pallas_call | solution.py:553
  369.4 1.7 shard_map.53

commit v3 on v2

--- a/solution.py
+++ b/solution.py
@@ -8,7 +8,7 @@
 from jax.sharding import PartitionSpec as P
 
 ITERS = 3
-AHEAD = 4
+AHEAD = 7
 LATE = 3
 HELD = 1
 

time: 371 us -> 371 us (level)
  no operation moved by 1% of the time
where the time goes in v3:
time: 371 us
  Pallas kernels  370 us (100%)
    pallas_call x1, Pallas kernels, step_direct(): pl.pallas_call(functools.partial(step_kernel, n, models), out_shape=(pltp...  291 us
    pallas_call x1, Pallas kernels, step_direct(): pl.pallas_call(functools.partial(tail_kernel, n, per), out_shape=(pltpu.V...  72.9 us

profile of v3, /device:TPU:11, one launch (start us, length us, event | category | flops | bytes accessed | tf_op | source)
XLA Modules:
  0.0 371.0 jit_solution(16044343953650909902)
XLA Ops:
  0.6 290.7 %shard_map.50 = (f32[16,5,8,2048]{3,2,1,0:T(8,128)S(1)}, f32[16,8,8,2048]{3,2,1,0:T(8,128)S(1)}, f32[8,128,2048]{2,1,0:T(8,128)S(1)}) custom-call(f32[16,8,8,2048]{3,2,1,0:T(8,128)} %bitcast.7, f32[16,8,8,2048]{3,2,1,0:T(8,128)} %bitcast.8, f32[16,8,8,2048]{3,2,1,0:T(8,128)} %bitcast.5), custom_call_target="tpu_custom_call" | custom-call | tf_op jit(solution)/shard_map/pallas_call | solution.py:511
  291.4 5.0 %shard_map.51 = (f32[16,8,8,2048]{3,2,1,0:T(8,128)}, f32[16,8,8,2048]{3,2,1,0:T(8,128)}, f32[8,128]{1,0:T(8,128)S(1)}) custom-call(f32[16,5,8,2048]{3,2,1,0:T(8,128)S(1)} %get-tuple-element.10.out_ref, f32[16,8,8,2048]{3,2,1,0:T(8,128)S(1)} %get-tuple-element.11.new_ref), custom_call_target="tpu_custom_call" | custom-call | tf_op jit(solution)/shard_map/pallas_call | solution.py:545
  296.4 72.9 %shard_map.52 = (f32[16,3,8,2048]{3,2,1,0:T(8,128)S(1)}, f32[16,8,2048]{2,1,0:T(8,128)S(1)}) custom-call(f32[8,128,2048]{2,1,0:T(8,128)S(1)} %get-tuple-element.13.x, f32[16,8,8,2048]{3,2,1,0:T(8,128)} %bitcast.6, f32[8,128]{1,0:T(8,128)S(1)} %get-tuple-element.14.token_ref), custom_call_target="tpu_custom_call" | custom-call | tf_op jit(solution)/shard_map/pallas_call | solution.py:553
  369.3 1.7 shard_map.53
